TPU v7x, 16 devices: a 4x2x1 block of a 4x4x8 slice. The times are simulated.
16 devices in a mesh: dp: 2 (over y, z), tp: 8 (over x, core).
Axes of the slice: x: 4, y: 2, z: 1, core: 2. Of those that a mesh axis runs over, the one named last changes fastest.
The devices are a block of a 4x4x8 slice.
Arguments:
- x_in: bfloat16 [24, 1024, 2048], P('dp'), parts along dimension 0
- seq_lens: int32 [24], P('dp'), parts along dimension 0
- ln1_gain: float32 [2048], replicated
- ln1_bias: float32 [2048], replicated
- w_qkv: bfloat16 [2048, 3, 32, 64], P(None, None, 'tp')
- b_qkv: bfloat16 [3, 32, 64], P(None, 'tp')
- w_out: bfloat16 [32, 64, 2048], P('tp')
- b_out: bfloat16 [2048], replicated
- ln2_gain: float32 [2048], replicated
- ln2_bias: float32 [2048], replicated
- w_up: bfloat16 [2048, 8192], P(None, 'tp')
- b_up: bfloat16 [8192], P('tp')
- w_down: bfloat16 [8192, 2048], P('tp')
- b_down: bfloat16 [2048], replicated
Outputs:
- output 1: bfloat16 [24, 1024, 2048], P('dp'), parts along dimension 0
- output 2: bfloat16 [24, 32, 1024, 64], P('dp', 'tp'), parts along dimension 0
- output 3: bfloat16 [24, 32, 1024, 64], P('dp', 'tp'), parts along dimension 0
There are 2 independent parts. A program takes and returns all parts, laid end to end along the dimension named above; an argument that names none is the same for every part.
All inputs are finite; a program needn't handle non-finite values.
Results may differ from a plain program's by a relative error of at most 0.0134191.
Values are sent between devices in bfloat16 or wider.
A program may use at most 768 MiB of HBM per device.

v0:
```python
import jax
import jax.numpy as jnp
from jax import lax
from jax.sharding import PartitionSpec as P


def layer_norm(values, gain_vec, bias_vec):
    values = values.astype(jnp.float32)
    row_mean = jnp.mean(values, axis=-1, keepdims=True)
    centered = values - row_mean
    row_var = jnp.mean(centered * centered, axis=-1, keepdims=True)
    return (centered * lax.rsqrt(row_var + 1e-5) * gain_vec + bias_vec).astype(jnp.bfloat16)


def cache_keep(values, seq_lens):
    positions = jnp.arange(values.shape[2])
    valid = positions[None, None, :, None] < seq_lens[:, None, None, None]
    return jnp.where(valid, values, 0)


def causal_mask(seq_lens, seq_len):
    positions = jnp.arange(seq_len)
    causal = positions[None, :] <= positions[:, None]
    in_length = positions[None, None, None, :] < seq_lens[:, None, None, None]
    return causal[None, None] & in_length


def attend(q_all, k_all, v_all, allowed):
    score_scale = q_all.shape[-1] ** -0.5
    scores = jnp.einsum("bhqk,bhsk->bhqs", q_all, k_all, preferred_element_type=jnp.float32) * score_scale
    scores = jnp.where(allowed, scores, -1e30)
    attn_probs = jax.nn.softmax(scores, axis=-1).astype(jnp.bfloat16)
    return jnp.einsum("bhqs,bhsk->bhqk", attn_probs, v_all, preferred_element_type=jnp.float32).astype(jnp.bfloat16)


def solution(mesh):
    def local_layer(x_in, seq_lens, ln1_gain, ln1_bias, w_qkv, b_qkv, w_out, b_out, ln2_gain, ln2_bias, w_up, b_up, w_down, b_down):
        normed = layer_norm(x_in, ln1_gain, ln1_bias)
        qkv_all = jnp.einsum("bsd,dthk->tbhsk", normed, w_qkv, preferred_element_type=jnp.float32)
        qkv_all = (qkv_all + b_qkv.astype(jnp.float32)[:, None, :, None, :]).astype(jnp.bfloat16)
        allowed = causal_mask(seq_lens, x_in.shape[1])
        attended = attend(qkv_all[0], qkv_all[1], qkv_all[2], allowed)
        part_out = jnp.einsum("cirl,ile->cre", attended, w_out, preferred_element_type=jnp.float32).astype(jnp.bfloat16)
        summed_out = lax.psum(part_out, "tp")
        x_mid = (x_in.astype(jnp.float32) + summed_out.astype(jnp.float32) + b_out.astype(jnp.float32)).astype(jnp.bfloat16)
        normed2 = layer_norm(x_mid, ln2_gain, ln2_bias)
        up_proj = jnp.einsum("bsd,df->bsf", normed2, w_up, preferred_element_type=jnp.float32) + b_up.astype(jnp.float32)
        hidden = jax.nn.relu(up_proj).astype(jnp.bfloat16)
        part_down = jnp.einsum("bsf,fd->bsd", hidden, w_down, preferred_element_type=jnp.float32).astype(jnp.bfloat16)
        summed_down = lax.psum(part_down, "tp")
        x_out = (x_mid.astype(jnp.float32) + summed_down.astype(jnp.float32) + b_down.astype(jnp.float32)).astype(jnp.bfloat16)
        return x_out, cache_keep(qkv_all[1], seq_lens), cache_keep(qkv_all[2], seq_lens)

    arg_specs = (P("dp", None, None), P("dp"), P(), P(), P(None, None, "tp", None), P(None, "tp", None), P("tp", None, None), P(), P(), P(), P(None, "tp"), P("tp"), P("tp", None), P())
    cache_spec = P("dp", "tp", None, None)
    result_specs = (P("dp", None, None), cache_spec, cache_spec)
    return jax.shard_map(local_layer, mesh=mesh, in_specs=arg_specs, out_specs=result_specs, check_vma=False)
```

profile of v0, /device:TPU:113, one launch (start us, length us, event | category | flops | bytes accessed | tf_op | source)
XLA Modules:
  0.0 1490.4 jit_solution(15360962086992874902)
XLA Ops:
  7.2 0.1 all-reduce.3.cloned.1.call-start
  7.3 0.3 iota_compare_fusion
  7.6 16.3 %convert_reduce_fusion.1 = f32[12,1024]{1,0:T(8,128)S(1)} fusion(bf16[12,1024,2048]{2,1,0:T(8,128)(2,1)} %param.14), kind=kLoop, calls=%fused_computation.10 | loop fusion | flops 50319360 | bytes 50380800 | tf_op jit(solution)/shard_map/reduce_sum | solution.py:9
  23.9 18.5 %fusion.10 = f32[12,1024]{1,0:T(8,128)S(1)} fusion(bf16[12,1024,2048]{2,1,0:T(8,128)(2,1)} %param.14, f32[12,1024]{1,0:T(8,128)S(1)} %broadcast_multiply_fusion.1), kind=kLoop, calls=%fused_computation.19 | loop fusion | flops 100651008 | bytes 50429952 | tf_op jit(solution)/shard_map/reduce_sum | solution.py:11
  42.5 0.1 iota_compare_fusion.1
  42.6 0.6 copy-done.2
  43.2 7.8 broadcast_and_fusion
  51.0 46.7 %fusion.35 = bf16[3,12,4,1024,64]{3,4,2,0,1:T(8,128)(2,1)} fusion(f32[3,4,64]{2,1,0:T(4,128)S(1)} %convert_element_type.64, bf16[12,1024,2048]{2,1,0:T(8,128)(2,1)} %param.14, f32[2048]{0:T(1024)S(1)} %copy-done.12, f32[2048]{0:T(1024)S(1)} %copy-done.13, f32[12,1024]{1,0:T(8,128)S(1)} %add_rsqrt_fusion.1, f32[12,1024]{1,0:T(8,128)S(1)} %broadcast_multiply_fusion.1, ...), kind=kOutput, calls=%fused_computation.46 | convolution fusion | flops 38824574976 | bytes 72469504 | tf_op jit(solution)/shard_map/bsd,dthk->tbhsk/dot_general | solution.py:39
  97.8 82.6 %fusion.48 = (f32[12,4,1024]{2,1,0:T(4,128)S(1)}, f32[12,4,1024,1024]{2,3,1,0:T(8,128)}) fusion(pred[12,1024,1024]{1,2,0:T(8,128)(4,1)} %broadcast_and_fusion, bf16[3,12,4,1024,64]{3,4,2,0,1:T(8,128)(2,1)} %fusion.35), kind=kOutput, calls=%fused_computation.67 | convolution fusion | flops 6643778560 | bytes 226689024 | tf_op jit(solution)/shard_map/sub | solution.py:32
  180.4 81.7 %bitcast_convert_fusion = bf16[12,1024,2048]{2,1,0:T(8,128)(2,1)} fusion(f32[12,4,1024,1024]{2,3,1,0:T(8,128)} %get-tuple-element.8, f32[12,4,1024]{2,1,0:T(4,128)S(1)} %get-tuple-element.7, bf16[3,12,4,1024,64]{3,4,2,0,1:T(8,128)(2,1)} %fusion.35, bf16[4,64,2048]{2,1,0:T(8,128)(2,1)S(1)} %copy-done.11), kind=kOutput, calls=%fused_computation.27 | convolution fusion | flops 19456327680 | bytes 259194880 | tf_op jit(solution)/shard_map/cirl,ile->cre/dot_general | solution.py:43
  262.1 0.1 all-reduce.3.cloned.1.call-update
  262.1 0.1 all-reduce.5.cloned.1.call-start
  262.2 0.5 copy-done.4
  262.8 0.6 convert_element_type.75
  263.4 491.0 %all-reduce.3.cloned.1.call-done = bf16[12,1024,2048]{2,1,0:T(8,128)(2,1)} async-done(((bf16[12,1024,2048]{2,1,0:T(8,128)(2,1)}), bf16[12,1024,2048]{2,1,0:T(8,128)(2,1)}) %all-reduce.3.cloned.1.call-update) | async-done | bytes 50331664 | tf_op jit(solution)/shard_map/psum | solution.py:44
  754.4 49.7 %convert_reduce_fusion = (f32[12,1024]{1,0:T(8,128)S(1)}, bf16[12,1024,2048]{2,1,0:T(8,128)(2,1)}) fusion(f32[2048]{0:T(1024)S(1)} %convert_element_type.71, bf16[12,1024,2048]{2,1,0:T(8,128)(2,1)} %all-reduce.3.cloned.1.call-done, bf16[12,1024,2048]{2,1,0:T(8,128)(2,1)} %param.14), kind=kLoop, calls=%fused_computation.7 | loop fusion | flops 176148480 | bytes 151052288 | tf_op jit(solution)/shard_map/reduce_sum | solution.py:9
  804.1 18.7 %fusion.6 = f32[12,1024]{1,0:T(8,128)S(1)} fusion(bf16[12,1024,2048]{2,1,0:T(8,128)(2,1)} %get-tuple-element.4, f32[12,1024]{1,0:T(8,128)S(1)} %broadcast_multiply_fusion), kind=kLoop, calls=%fused_computation.15 | loop fusion | flops 100651008 | bytes 50429952 | tf_op jit(solution)/shard_map/reduce_sum | solution.py:11
  822.9 60.6 %fusion.23 = f32[12,1024,1024]{2,1,0:T(8,128)} fusion(bf16[12,1024,2048]{2,1,0:T(8,128)(2,1)} %get-tuple-element.4, f32[2048]{0:T(1024)S(1)} %copy-done.14, f32[2048]{0:T(1024)S(1)} %copy-done.15, f32[12,1024]{1,0:T(8,128)S(1)} %add_rsqrt_fusion, f32[12,1024]{1,0:T(8,128)S(1)} %broadcast_multiply_fusion, bf16[2048,1024]{1,0:T(8,128)(2,1)S(1)} %copy-done.10), kind=kOutput, calls=%fused_computation.33 | convolution fusion | flops 51690602496 | bytes 104972288 | tf_op jit(solution)/shard_map/bsd,df->bsf/dot_general | solution.py:47
  883.5 61.2 %convolution_convert_fusion = bf16[12,1024,2048]{2,1,0:T(8,128)(2,1)} fusion(f32[12,1024,1024]{2,1,0:T(8,128)} %fusion.23, f32[1024]{0:T(1024)S(1)} %copy-done.6, bf16[1024,2048]{1,0:T(8,128)(2,1)} %param.26), kind=kOutput, calls=%fused_computation.41 | convolution fusion | flops 51602522112 | bytes 104861696 | tf_op jit(solution)/shard_map/bsf,fd->bsd/dot_general | solution.py:49
  944.7 0.1 all-reduce.5.cloned.1.call-update
  944.8 0.6 copy-done.5
  945.4 10.3 broadcast_select_fusion
  955.7 478.5 %all-reduce.5.cloned.1.call-done = bf16[12,1024,2048]{2,1,0:T(8,128)(2,1)} async-done(((bf16[12,1024,2048]{2,1,0:T(8,128)(2,1)}), bf16[12,1024,2048]{2,1,0:T(8,128)(2,1)}) %all-reduce.5.cloned.1.call-update) | async-done | bytes 50331664 | tf_op jit(solution)/shard_map/psum | solution.py:50
  1434.2 49.2 %fusion.17 = bf16[12,1024,2048]{2,1,0:T(8,128)(2,1)} fusion(bf16[12,1024,2048]{2,1,0:T(8,128)(2,1)} %get-tuple-element.4, bf16[12,1024,2048]{2,1,0:T(8,128)(2,1)} %all-reduce.5.cloned.1.call-done, f32[2048]{0:T(1024)S(1)} %convert_element_type.79), kind=kLoop, calls=%fused_computation.26 | loop fusion | flops 125829120 | bytes 151003136 | tf_op jit(solution)/shard_map/convert_element_type | solution.py:51
  (36 shorter events, 0.2 us)
Async XLA Ops:
  7.2 43.8 %copy-start = (bf16[2048,3,4,64]{0,3,2,1:T(8,128)(2,1)S(1)}, bf16[2048,3,4,64]{0,3,2,1:T(8,128)(2,1)}, u32[]{:S(2)}) copy-start(bf16[2048,3,4,64]{0,3,2,1:T(8,128)(2,1)} %param.18) | copy-start | bytes 9437188
  7.2 747.2 %all-reduce.3.cloned.1.call-start = ((), (), s32[]{:S(2)}) async-start(), calls=%async_computation | async-start | bytes 100663296 | tf_op jit(solution)/shard_map/psum | solution.py:44
  7.6 34.9 %copy-start.7 = (bf16[3,4,64]{2,1,0:T(4,128)(2,1)S(1)}, bf16[3,4,64]{2,1,0:T(4,128)(2,1)}, u32[]{:S(2)}) copy-start(bf16[3,4,64]{2,1,0:T(4,128)(2,1)} %param.19) | copy-start | bytes 4612
  7.6 34.9 %copy-start.9 = (s32[12]{0:T(128)S(1)}, s32[12]{0:T(128)}, u32[]{:S(2)}) copy-start(s32[12]{0:T(128)} %param.15) | copy-start | bytes 148
  7.6 43.4 %copy-start.12 = (f32[2048]{0:T(1024)S(1)}, f32[2048]{0:T(1024)}, u32[]{:S(2)}) copy-start(f32[2048]{0:T(1024)} %param.17) | copy-start | bytes 24580
  7.6 43.4 %copy-start.13 = (f32[2048]{0:T(1024)S(1)}, f32[2048]{0:T(1024)}, u32[]{:S(2)}) copy-start(f32[2048]{0:T(1024)} %param.16) | copy-start | bytes 24580
  42.6 0.6 copy-start.2
  97.8 82.6 %copy-start.11 = (bf16[4,64,2048]{2,1,0:T(8,128)(2,1)S(1)}, bf16[4,64,2048]{2,1,0:T(8,128)(2,1)}, u32[]{:S(2)}) copy-start(bf16[4,64,2048]{2,1,0:T(8,128)(2,1)} %param.20) | copy-start | bytes 3145732
  262.1 0.7 copy-start.4
  262.1 0.7 copy-start.8
  262.1 1172.1 %all-reduce.5.cloned.1.call-start = ((), (), s32[]{:S(2)}) async-start(), calls=%async_computation.1 | async-start | bytes 100663296 | tf_op jit(solution)/shard_map/psum | solution.py:50
  804.1 18.8 %copy-start.10 = (bf16[2048,1024]{1,0:T(8,128)(2,1)S(1)}, bf16[2048,1024]{1,0:T(8,128)(2,1)}, u32[]{:S(2)}) copy-start(bf16[2048,1024]{1,0:T(8,128)(2,1)} %param.24) | copy-start | bytes 12582916
  804.1 18.8 %copy-start.14 = (f32[2048]{0:T(1024)S(1)}, f32[2048]{0:T(1024)}, u32[]{:S(2)}) copy-start(f32[2048]{0:T(1024)} %param.23) | copy-start | bytes 24580
  804.1 18.8 %copy-start.15 = (f32[2048]{0:T(1024)S(1)}, f32[2048]{0:T(1024)}, u32[]{:S(2)}) copy-start(f32[2048]{0:T(1024)} %param.22) | copy-start | bytes 24580
  822.9 60.6 %copy-start.6 = (f32[1024]{0:T(1024)S(1)}, f32[1024]{0:T(1024)}, u32[]{:S(2)}) copy-start(f32[1024]{0:T(1024)} %convert_element_type.75) | copy-start | bytes 12292
  944.7 0.7 copy-start.5
  944.7 0.7 copy-start.3
  945.4 538.0 %copy-start.1 = (bf16[2048,3,4,64]{0,3,2,1:T(8,128)(2,1)S(1)}, bf16[2048,3,4,64]{0,3,2,1:T(8,128)(2,1)}, u32[]{:S(2)}) copy-start(bf16[2048,3,4,64]{0,3,2,1:T(8,128)(2,1)} %param.18) | copy-start | bytes 9437188
Sparse Core Ops, SparseCore 0:
  262.3 492.0 all-reduce.2
  944.9 489.2 all-reduce.4
where the time goes:
time: 1490 us
  waiting for transfers between devices  970 us (65%)
  matrix products  333 us (22%)
  other arithmetic  172 us (12%)
    psum x1, waiting for transfers between devices, local_layer(): summed_out = lax.psum(part_out, 'tp')  491 us
    psum x1, waiting for transfers between devices, local_layer(): summed_down = lax.psum(part_down, 'tp')  478 us
    sub x1, matrix products, attend(): attn_probs = jax.nn.softmax(scores, axis=-1).astype(jnp.bfloat16)  82.6 us
    dot_general x1, matrix products, local_layer(): jnp.einsum('cirl,ile->cre', attended, w_out, preferred_element_type=jnp.f...  81.7 us
    reduce_sum x2, other arithmetic, layer_norm(): row_mean = jnp.mean(values, axis=-1, keepdims=True)  66 us
    dot_general x1, matrix products, local_layer(): jnp.einsum('bsf,fd->bsd', hidden, w_down, preferred_element_type=jnp.floa...  61.2 us
    dot_general x1, matrix products, local_layer(): jnp.einsum('bsd,df->bsf', normed2, w_up, preferred_element_type=jnp.float32)  60.6 us
    convert_element_type x1, other arithmetic, local_layer(): (x_mid.astype(jnp.float32) + summed_down.astype(jnp.float32) + b_down.ast...  49.2 us
  transfers between devices with their start and end apart: 2, of which 2 were waited for; matrix products, arithmetic and copies ran while one was open for 1% of the time, Pallas kernels for 0%

commit v1 on v0

v1 whole, which is shorter than its diff:
```python
import functools
import math

import jax
import jax.numpy as jnp
from jax import lax
from jax.experimental import pallas as pl
from jax.experimental.pallas import tpu as pltpu
from jax.sharding import PartitionSpec as P

F32 = jnp.float32
BF16 = jnp.bfloat16
NT = (((1,), (1,)), ((), ()))

def k1_body(hd, lens_ref, x_ref, g_ref, bt_ref, wt_ref, bq_ref, bkv_ref, a_ref, kc_ref, vc_ref, h_scr, q_scr, ka_scr, kb_scr, *, b0, ln_rows, qt, unroll=1):
    seq, d = x_ref.shape
    width = a_ref.shape[-1]
    n_heads = width // hd
    length = lens_ref[pl.program_id(0) + b0]

    @pl.loop(0, seq // ln_rows, unroll=unroll)
    def _(r):
        rows = pl.ds(pl.multiple_of(r * ln_rows, ln_rows), ln_rows)
        x = x_ref[rows, :].astype(F32)
        mu = jnp.mean(x, axis=-1, keepdims=True)
        c = x - mu
        var = jnp.mean(c * c, axis=-1, keepdims=True)
        h_scr[rows, :] = (c * lax.rsqrt(var + 1e-5) * g_ref[...] + bt_ref[...]).astype(BF16)

    q = lax.dot_general(h_scr[...], wt_ref[:width, :], NT, preferred_element_type=F32)
    q_scr[...] = (q + bq_ref[...]).astype(BF16)
    keep = lax.broadcasted_iota(jnp.int32, (width, seq), 1) < length
    kt = lax.dot_general(wt_ref[width:2 * width, :], h_scr[...], NT, preferred_element_type=F32)
    kt = jnp.where(keep, kt + bkv_ref[:width, :], 0.0).astype(BF16)
    kc_ref[...] = kt
    row = lax.broadcasted_iota(jnp.int32, (width, seq), 0)
    bias = jnp.where(keep, 0.0, -1e30).astype(BF16)
    ka_scr[...] = jnp.where(row == width - 1, bias, kt)
    kb_scr[...] = jnp.where(row == 0, bias, kt)
    vt = lax.dot_general(wt_ref[2 * width:, :], h_scr[...], NT, preferred_element_type=F32)
    vc_ref[...] = jnp.where(keep, vt + bkv_ref[width:, :], 0.0).astype(BF16)

    c2 = hd ** -0.5 * math.log2(math.e)
    lane = lax.broadcasted_iota(jnp.int32, (qt, width), 1)
    causal = lax.broadcasted_iota(jnp.int32, (qt, qt), 1) <= lax.broadcasted_iota(jnp.int32, (qt, qt), 0)
    for i in range(seq // qt):
        span = (i + 1) * qt
        q_tile = q_scr[i * qt:(i + 1) * qt, :]
        out = jnp.zeros((qt, width), F32)
        for h in range(n_heads):
            low = h < n_heads // 2
            mine = (lane >= h * hd) & (lane < (h + 1) * hd)
            flag = lane == (width - 1 if low else 0)
            qm = jnp.where(mine, q_tile, jnp.where(flag, 1.0, 0.0).astype(BF16))
            k_src = ka_scr if low else kb_scr
            s = jnp.dot(qm, k_src[:, :span], preferred_element_type=F32)
            s_diag = jnp.where(causal, s[:, span - qt:], -1e30)
            s = jnp.concatenate([s[:, :span - qt], s_diag], axis=1) if i else s_diag
            m = jnp.max(s, axis=-1, keepdims=True)
            p = jnp.exp2((s - m) * c2)
            l = jnp.sum(p, axis=-1, keepdims=True)
            p = (p * (1.0 / l)).astype(BF16)
            pv = lax.dot_general(p, vc_ref[:, :span], NT, preferred_element_type=F32)
            out = jnp.where(mine, pv, out)
        a_ref[i * qt:(i + 1) * qt, :] = out.astype(BF16)

def k1(x_in, seq_lens, g, bt, w_qkv, b_qkv, *, ln_rows=64, qt=256, unroll=1, vmem=60 * 2**20):
    nb, seq, d = x_in.shape
    _, _, nh, hd = w_qkv.shape
    width = nh * hd
    wt = jnp.transpose(w_qkv, (1, 2, 3, 0)).reshape(3 * width, d)
    bq = b_qkv.astype(F32).reshape(3, width)
    full = lambda *shape: pl.BlockSpec(shape, lambda b, lens: (0,) * len(shape))
    per = lambda *shape: pl.BlockSpec((None,) + shape, lambda b, lens: (b,) + (0,) * len(shape))
    a, kc, vc = pl.pallas_call(
        functools.partial(k1_body, hd, b0=0, ln_rows=ln_rows, qt=qt, unroll=unroll),
        out_shape=[jax.ShapeDtypeStruct((nb, seq, width), BF16)] + [jax.ShapeDtypeStruct((nb, width, seq), BF16)] * 2,
        grid_spec=pltpu.PrefetchScalarGridSpec(
            num_scalar_prefetch=1, grid=(nb,),
            in_specs=[per(seq, d), full(1, d), full(1, d), full(3 * width, d), full(1, width), full(2 * width, 1)],
            out_specs=[per(seq, width), per(width, seq), per(width, seq)],
            scratch_shapes=[pltpu.VMEM((seq, d), BF16), pltpu.VMEM((seq, width), BF16), pltpu.VMEM((width, seq), BF16), pltpu.VMEM((width, seq), BF16)],
        ),
        compiler_params=pltpu.CompilerParams(vmem_limit_bytes=vmem),
        cost_estimate=pl.CostEstimate(flops=2 * nb * seq * d * 3 * width + 2 * nb * seq * seq * width, bytes_accessed=2 * nb * seq * (d + 3 * width), transcendentals=nb * nh * seq * seq // 2),
    )(seq_lens, x_in, g.reshape(1, d), bt.reshape(1, d), wt, bq[:1], bq[1:].reshape(2 * width, 1))
    un = lambda t: jnp.transpose(t.reshape(nb, nh, hd, seq), (0, 1, 3, 2))
    return a, un(kc), un(vc)

def k2_body(n, a_ref, x_ref, wu_in, wd_in, wo_in, flu, fld, flo, fru, frd, fro, bup_ref, g_ref, bt_ref, bo_ref, bd_ref,
            out_ref, aall, wu, wd, wo,
            acc, h2, stage, ubuf, wub, wdb, abuf, wob, bups,
            send_sems, recv_sems, sem_u, sem_d, sem_a, sem_o, sem_x, sem_g):
    nb, seq, d = x_ref.shape
    ff = wu_in.shape[1]
    width = a_ref.shape[-1]
    rb = seq // n
    hb = nb // 2
    half_rows = hb * rb
    me = lax.axis_index("tp")
    dp = lax.axis_index("dp")
    par = lax.rem(dp, 2)
    core = lax.rem(me, 2)
    flip = 1 - 2 * core
    rgt, lft, opp = lax.rem(me + 2, n), lax.rem(me + n - 2, n), lax.rem(me + n // 2, n)
    sib, lft2, rgt2, opp2 = me + flip, lft + flip, rgt + flip, opp + flip
    to_r, to_l, to_s = {"tp": rgt}, {"tp": lft}, {"tp": sib}
    to_p = {"dp": dp + 1 - 2 * par}

    count = [0]
    copies, got = [], set()

    def remote(src, dst, target):
        i = count[0]
        count[0] += 1
        c = pltpu.make_async_remote_copy(src_ref=src, dst_ref=dst, send_sem=send_sems.at[i], recv_sem=recv_sems.at[i], device_id=target, device_id_type=pl.DeviceIdType.MESH)
        c.start()
        copies.append(c)
        return c

    def ensure(*cs):
        for c in cs:
            if id(c) not in got:
                got.add(id(c))
                c.wait_recv()

    barrier = pltpu.get_barrier_semaphore()
    for r in range(1, n):
        pl.semaphore_signal(barrier, inc=1, device_id={"tp": lax.rem(me + r, n)}, device_id_type=pl.DeviceIdType.MESH)
    pl.semaphore_signal(barrier, inc=1, device_id=to_p, device_id_type=pl.DeviceIdType.MESH)
    pl.semaphore_wait(barrier, n)

    ku, kd, ko = d // 2, ff // 2, width
    qu, qd = d // 4, ff // 4
    cu, cd = pl.multiple_of(ku + par * qu, qu), pl.multiple_of(kd + par * qd, qd)
    eu, ed = pl.multiple_of(ku + (1 - par) * qu, qu), pl.multiple_of(kd + (1 - par) * qd, qd)

    def x_copy(h):
        rows = pl.ds(pl.multiple_of(me * rb, rb), rb)
        return pltpu.make_async_copy(x_ref.at[h * hb:(h + 1) * hb, rows, :], stage.at[h], sem_x.at[h])
    x_copies = [x_copy(0), x_copy(1)]
    x_copies[0].start()

    a2a = {}
    def send_a(h):
        for r in (2, n - 2, 3, n - 3, 4, 5, 1) if n == 8 else range(1, n):
            pass
        for r in sorted(range(1, n)):
            t = lax.rem(me + r, n)
            a2a[h, r] = remote(a_ref.at[h * hb:(h + 1) * hb, pl.ds(pl.multiple_of(t * rb, rb), rb), :], aall.at[h, me], {"tp": t})
    send_a(0)
    bup = [remote(bup_ref, bups.at[me], {"tp": lax.rem(me + r, n)}) for r in range(1, n)]
    bups[me] = bup_ref[...]
    s_wo = remote(wo_in, wo.at[me], to_s)
    s_lo = remote(flo, wo.at[lft], to_s)
    s_ro = remote(fro, wo.at[rgt], to_s)
    f_o = [remote(flo.at[:ko // 2], wo.at[lft, :ko // 2], to_r), remote(fro.at[ko // 2:], wo.at[rgt, ko // 2:], to_l)]
    p_lu = remote(flu.at[ku:], wu.at[lft, pl.ds(cu, qu)], to_p)
    p_ld = remote(fld.at[kd:], wd.at[lft, pl.ds(cd, qd)], to_p)
    p_ru = remote(fru.at[ku:], wu.at[rgt, pl.ds(cu, qu)], to_p)
    p_rd = remote(frd.at[kd:], wd.at[rgt, pl.ds(cd, qd)], to_p)
    f_cu = [remote(flu.at[ku:ku + qu // 2], wu.at[lft, pl.ds(cu, qu // 2)], to_r),
            remote(fru.at[ku + qu // 2:], wu.at[rgt, pl.ds(cu + qu // 2, qu // 2)], to_l)]
    f_cd = [remote(fld.at[kd:kd + qd // 2], wd.at[lft, pl.ds(cd, qd // 2)], to_r),
            remote(frd.at[kd + qd // 2:], wd.at[rgt, pl.ds(cd + qd // 2, qd // 2)], to_l)]
    send_a(1)
    f_uu = [remote(flu.at[:ku // 2], wu.at[lft, :ku // 2], to_r), remote(fru.at[ku // 2:ku], wu.at[rgt, ku // 2:ku], to_l)]
    f_ud = [remote(fld.at[:kd // 2], wd.at[lft, :kd // 2], to_r), remote(frd.at[kd // 2:kd], wd.at[rgt, kd // 2:kd], to_l)]
    s_own = [remote(wu_in, wu.at[me], to_s), remote(wd_in, wd.at[me], to_s)]
    s_l = [remote(flu.at[:ku], wu.at[lft, :ku], to_s), remote(flu.at[ku:], wu.at[lft, pl.ds(cu, qu)], to_s),
           remote(fld.at[:kd], wd.at[lft, :kd], to_s), remote(fld.at[kd:], wd.at[lft, pl.ds(cd, qd)], to_s)]
    s_r = [remote(fru.at[:ku], wu.at[rgt, :ku], to_s), remote(fru.at[ku:], wu.at[rgt, pl.ds(cu, qu)], to_s),
           remote(frd.at[:kd], wd.at[rgt, :kd], to_s), remote(frd.at[kd:], wd.at[rgt, pl.ds(cd, qd)], to_s)]
    x_copies[1].start()

    done = {}
    def on_pair(name, slot, cu_copy, cd_copy):
        if name in done:
            return
        ensure(cu_copy)
        one = remote(wu.at[slot, pl.ds(eu, qu)], wu.at[slot, pl.ds(eu, qu)], to_s)
        ensure(cd_copy)
        done[name] = [one, remote(wd.at[slot, pl.ds(ed, qd)], wd.at[slot, pl.ds(ed, qd)], to_s)]
    def on_opp_o():
        ensure(*f_o)
        done["opp_o"] = [remote(wo.at[opp], wo.at[opp], to_s)]
    def on_opp_c():
        ensure(*f_cu)
        done["p_ou"] = remote(wu.at[opp, pl.ds(cu, qu)], wu.at[opp, pl.ds(cu, qu)], to_p)
        s1 = remote(wu.at[opp, pl.ds(cu, qu)], wu.at[opp, pl.ds(cu, qu)], to_s)
        ensure(*f_cd)
        done["p_od"] = remote(wd.at[opp, pl.ds(cd, qd)], wd.at[opp, pl.ds(cd, qd)], to_p)
        done["opp_c"] = [s1, remote(wd.at[opp, pl.ds(cd, qd)], wd.at[opp, pl.ds(cd, qd)], to_s)]
    def on_opp_u():
        ensure(*f_uu)
        s1 = remote(wu.at[opp, :ku], wu.at[opp, :ku], to_s)
        ensure(*f_ud)
        done["opp_u"] = [s1, remote(wd.at[opp, :kd], wd.at[opp, :kd], to_s)]
    ev_pair_l = lambda: on_pair("pair_l", lft, p_lu, p_ld)
    ev_pair_r = lambda: on_pair("pair_r", rgt, p_ru, p_rd)
    ev_pair_o = lambda: on_pair("pair_o", opp, done["p_ou"], done["p_od"])

    def load(place, slot):
        u, dn = wub.at[slot], wdb.at[slot]
        if place == "own":
            parts = [(wu_in, u, sem_u), (wd_in, dn, sem_d)]
        elif place in ("lft", "rgt"):
            fu, fd, at = (flu, fld, lft) if place == "lft" else (fru, frd, rgt)
            ensure(*((p_lu, p_ld) if place == "lft" else (p_ru, p_rd)))
            parts = [(fu.at[:ku], u.at[:ku], sem_u), (fu.at[ku:], u.at[pl.ds(cu, qu)], sem_u), (wu.at[at, pl.ds(eu, qu)], u.at[pl.ds(eu, qu)], sem_u),
                     (fd.at[:kd], dn.at[:kd], sem_d), (fd.at[kd:], dn.at[pl.ds(cd, qd)], sem_d), (wd.at[at, pl.ds(ed, qd)], dn.at[pl.ds(ed, qd)], sem_d)]
        else:
            need = {"sib": s_own, "lft2": s_l + done.get("pair_l", []), "rgt2": s_r + done.get("pair_r", []), "opp": [], "opp2": []}[place]
            if place == "opp":
                need = f_uu + f_ud + f_cu + f_cd + [done["p_ou"], done["p_od"]]
            if place == "opp2":
                need = done["opp_c"] + done["opp_u"] + done["pair_o"]
            ensure(*need)
            at = {"sib": sib, "lft2": lft2, "rgt2": rgt2, "opp": opp, "opp2": opp2}[place]
            parts = [(wu.at[at], u, sem_u), (wd.at[at], dn, sem_d)]
        for src, dst, sem in parts:
            pltpu.make_async_copy(src, dst, sem.at[slot]).start()

    idx = {"own": me, "sib": sib, "lft": lft, "lft2": lft2, "rgt": rgt, "rgt2": rgt2, "opp": opp, "opp2": opp2}
    tile = 256

    def mlp(h, place, slot):
        pltpu.make_async_copy(wu.at[0], wub.at[slot], sem_u.at[slot]).wait()
        at = idx[place]
        @pl.loop(0, ff // tile)
        def _(i):
            cols = pl.ds(pl.multiple_of(i * tile, tile), tile)
            u = jnp.dot(h2[h], wub[slot, :, cols], preferred_element_type=F32)
            ubuf[:, cols] = jnp.maximum(u + bups[at, 0:1, cols], 0.0).astype(BF16)
        pltpu.make_async_copy(wd.at[0], wdb.at[slot], sem_d.at[slot]).wait()
        @pl.loop(0, d // tile)
        def _(i):
            cols = pl.ds(pl.multiple_of(i * tile, tile), tile)
            acc[h, :, cols] += jnp.dot(ubuf[...], wdb[slot, :, cols], preferred_element_type=F32)

    def load_a(h):
        rows = pl.ds(pl.multiple_of(me * rb, rb), rb)
        cs = [pltpu.make_async_copy(a_ref.at[h * hb:(h + 1) * hb, rows, :], abuf.at[:, :, pl.ds(pl.multiple_of(me * width, width), width)], sem_a.at[0])]
        cs[0].start()
        for r in range(1, n):
            ensure(a2a[h, r])
            j = lax.rem(me + n - r, n)
            c = pltpu.make_async_copy(aall.at[h, j], abuf.at[:, :, pl.ds(pl.multiple_of(j * width, width), width)], sem_a.at[r])
            c.start()
            cs.append(c)
        for c in cs:
            c.wait()

    def proj(h):
        x_copies[h].wait()
        @pl.loop(0, d // tile)
        def _(i):
            cols = pl.ds(pl.multiple_of(i * tile, tile), tile)
            o = jnp.dot(abuf[...].reshape(half_rows, n * width), wob[:, cols], preferred_element_type=F32)
            acc[h, :, cols] = o
        @pl.loop(0, hb)
        def _(b):
            rows = pl.ds(pl.multiple_of(b * rb, rb), rb)
            x1 = (stage[h, b].astype(F32) + acc[h, rows, :] + bo_ref[...]).astype(BF16).astype(F32)
            mu = jnp.mean(x1, axis=-1, keepdims=True)
            c = x1 - mu
            var = jnp.mean(c * c, axis=-1, keepdims=True)
            h2[h, rows, :] = (c * lax.rsqrt(var + 1e-5) * g_ref[...] + bt_ref[...]).astype(BF16)
            acc[h, rows, :] = x1 + bd_ref[...]

    def put_o(src, j, i):
        c = pltpu.make_async_copy(src, wob.at[pl.ds(pl.multiple_of(j * width, width), width)], sem_o.at[i])
        c.start()
        return c
    oc = [put_o(wo_in, me, 0), put_o(flo, lft, 1), put_o(fro, rgt, 2)]
    load("own", 0)
    ensure(s_wo); oc.append(put_o(wo.at[sib], sib, 3))
    ensure(s_lo); oc.append(put_o(wo.at[lft2], lft2, 4))
    ensure(s_ro); oc.append(put_o(wo.at[rgt2], rgt2, 5))
    load("sib", 1)
    ensure(*bup)
    on_opp_o()
    oc.append(put_o(wo.at[opp], opp, 6))
    load_a(0)
    ensure(*done["opp_o"]); oc.append(put_o(wo.at[opp2], opp2, 7))
    for c in oc:
        c.wait()
    proj(0)

    out_own = {}
    def finish(h):
        rows = pl.ds(pl.multiple_of(me * rb, rb), rb)
        for b in range(hb):
            stage[h, b] = acc[h, b * rb:(b + 1) * rb, :].astype(BF16)
        cut = hb // 2
        right = list(range(hb))
        left = right[cut:] + right[:cut]
        loc = pltpu.make_async_copy(stage.at[h], out_ref.at[h * hb:(h + 1) * hb, rows, :], sem_g.at[h])
        loc.start()
        for b1, b2 in zip(right, left):
            for b, to, key in ((b1, to_r, "r"), (b2, to_l, "l")):
                out_own[h, b, key] = remote(stage.at[h, b], out_ref.at[h * hb + b, rows, :], to)
        for b in range(hb):
            out_own[h, b, "s"] = remote(stage.at[h, b], out_ref.at[h * hb + b, rows, :], to_s)
        return loc

    fwd, sdone = {}, []
    def at_out(h, b, owner):
        return out_ref.at[h * hb + b, pl.ds(pl.multiple_of(owner * rb, rb), rb), :]
    def pass_on(h, b, key):
        owner, onward = (lft, to_r) if key == "r" else (rgt, to_l)
        ensure(out_own[h, b, key])
        if (b < hb // 2) == (key == "r"):
            fwd[h, b] = remote(at_out(h, b, owner), at_out(h, b, owner), onward)
        sdone.append(remote(at_out(h, b, owner), at_out(h, b, owner), to_s))
    def last(h, b):
        ensure(fwd[h, b])
        sdone.append(remote(at_out(h, b, opp), at_out(h, b, opp), to_s))

    tasks = [(0, "own"), (0, "sib"), (0, "lft"), (0, "lft2"), "proj1", (1, "own"), (1, "sib"), (1, "lft"), (1, "lft2"),
             (0, "rgt"), (0, "rgt2"), (1, "rgt"), (1, "rgt2"), (0, "opp"), (0, "opp2"), "fin0", (1, "opp"), "xo", (1, "opp2"), "fin1"]
    late = {(0, "lft"): [ev_pair_l], (0, "lft2"): [], (0, "rgt"): [on_opp_c, ev_pair_r], (0, "rgt2"): [], (0, "opp"): [ev_pair_o, on_opp_u], (0, "opp2"): []}
    slot = 0
    loaded = {0: (0, "own"), 1: (0, "sib")}
    order = [t for t in tasks if isinstance(t, tuple)]
    where = {order[0]: 0, order[1]: 1}
    nxt = 2
    locs = []
    def run_late(t):
        for e in late.get(t, []):
            e()
    def fetch(pos, s):
        t = order[pos]
        run_late(t)
        load(t[1], s)
        where[t] = s
    pos = 0
    for t in tasks:
        if t == "proj1":
            load_a(1)
            proj(1)
        elif t in ("fin0", "fin1"):
            locs.append(finish(int(t[-1])))
        elif t == "xo":
            pass_on(0, 0, "r")
            pass_on(0, hb // 2, "l")
        else:
            if t not in where:
                fetch(pos, pos % 2)
            mlp(t[0], t[1], where[t])
            if pos + 2 < len(order):
                nt = order[pos + 2]
                if nt not in late:
                    fetch(pos + 2, pos % 2)
            pos += 1
    cut = hb // 2
    for h in (0, 1):
        for i in range(cut):
            if (h, i) != (0, 0):
                pass_on(h, i, "r")
                pass_on(h, cut + i, "l")
        for i in range(cut):
            pass_on(h, cut + i, "r")
            pass_on(h, i, "l")
        if h == 1:
            for i in range(cut):
                last(0, i); last(0, cut + i)
    for i in range(cut):
        last(1, i); last(1, cut + i)
    for c in locs:
        c.wait()
    ensure(*copies)
    for c in copies:
        c.wait_send()

N_COPIES = 160

def k2(n, a, x_in, w_up, w_down, w_out, fl, fr, b_up, g, bt, b_out, b_down, *, vmem=63 * 2**20, ncopies=N_COPIES, cid=0):
    nb, seq, d = x_in.shape
    ff = w_up.shape[1]
    width = a.shape[-1]
    rb, hb = seq // n, nb // 2
    hr = rb * hb
    any_ = pl.BlockSpec(memory_space=pl.ANY)
    vm = pl.BlockSpec(memory_space=pltpu.VMEM)
    row = lambda t: t.astype(F32).reshape(1, -1)
    sds = jax.ShapeDtypeStruct
    outs = pl.pallas_call(
        functools.partial(k2_body, n),
        out_shape=[sds((nb, seq, d), BF16), sds((2, n, hb, rb, width), BF16), sds((n, d, ff), BF16), sds((n, ff, d), BF16), sds((n, width, d), BF16)],
        in_specs=[any_] * 11 + [vm] * 5,
        out_specs=[any_] * 5,
        scratch_shapes=[
            pltpu.VMEM((2, hr, d), F32), pltpu.VMEM((2, hr, d), BF16), pltpu.VMEM((2, hb, rb, d), BF16), pltpu.VMEM((hr, ff), BF16),
            pltpu.VMEM((2, d, ff), BF16), pltpu.VMEM((2, ff, d), BF16), pltpu.VMEM((hb, rb, n * width), BF16), pltpu.VMEM((n * width, d), BF16),
            pltpu.VMEM((n, 8, ff), F32),
            pltpu.SemaphoreType.DMA((ncopies,)), pltpu.SemaphoreType.DMA((ncopies,)),
            pltpu.SemaphoreType.DMA((2,)), pltpu.SemaphoreType.DMA((2,)), pltpu.SemaphoreType.DMA((n,)), pltpu.SemaphoreType.DMA((n,)),
            pltpu.SemaphoreType.DMA((2,)), pltpu.SemaphoreType.DMA((2,)),
        ],
        compiler_params=pltpu.CompilerParams(collective_id=cid, has_side_effects=True, vmem_limit_bytes=vmem),
        cost_estimate=pl.CostEstimate(flops=2 * nb * rb * d * (4 * ff * n + 2 * n * width) // 2, bytes_accessed=4 * n * d * ff * 2, transcendentals=0),
    )(a, x_in, w_up, w_down, w_out, *fl, *fr, jnp.broadcast_to(row(b_up), (8, ff)), row(g), row(bt), row(b_out), row(b_down))
    return outs[0]

def moved(n, dp_index, w_up, w_down, w_out):
    par = lax.rem(dp_index, 2)
    def block(w):
        q = w.shape[0] // 4
        return jnp.concatenate([w[:2 * q], lax.dynamic_slice_in_dim(w, (2 + par) * q, q, 0)], axis=0)
    parts = (block(w_up), block(w_down), w_out)
    right = [(i, (i + 2) % n) for i in range(n)]
    left = [(i, (i - 2) % n) for i in range(n)]
    fl = [lax.ppermute(t, "tp", right) for t in parts]
    fr = [lax.ppermute(t, "tp", left) for t in parts]
    return fl, fr


def solution(mesh):
    n = mesh.shape["tp"]

    def local_layer(x_in, seq_lens, ln1_gain, ln1_bias, w_qkv, b_qkv, w_out, b_out, ln2_gain, ln2_bias, w_up, b_up, w_down, b_down):
        w_o = w_out.reshape(-1, w_out.shape[-1])
        fl, fr = moved(n, lax.axis_index("dp"), w_up, w_down, w_o)
        a, k_cache, v_cache = k1(x_in, seq_lens, ln1_gain, ln1_bias, w_qkv, b_qkv, ln_rows=256, unroll=4)
        x_out = k2(n, a, x_in, w_up, w_down, w_o, fl, fr, b_up, ln2_gain, ln2_bias, b_out, b_down)
        return x_out, k_cache, v_cache

    arg_specs = (P("dp", None, None), P("dp"), P(), P(), P(None, None, "tp", None), P(None, "tp", None), P("tp", None, None), P(), P(), P(), P(None, "tp"), P("tp"), P("tp", None), P())
    cache_spec = P("dp", "tp", None, None)
    result_specs = (P("dp", None, None), cache_spec, cache_spec)
    return jax.shard_map(local_layer, mesh=mesh, in_specs=arg_specs, out_specs=result_specs, check_vma=False)
```

time: 1490 us -> 655 us (0.44)
  waiting for transfers between devices: 970 us -> 18.6 us
  Pallas kernels: 0 us -> 572 us
  matrix products: 333 us -> 0 us
  other arithmetic: 172 us -> 5.06 us
  local copies, waits for them, and re-layouts: 1.89 us -> 38.2 us
    psum x2 -> x0, waiting for transfers between devices: 970 us -> none  [the longest x1 491 us: local_layer(): summed_out = lax.psum(part_out, 'tp')]
    pallas_call x0 -> x2, Pallas kernels: none -> 572 us  [the longest x1 446 us: k2(): pl.pallas_call(functools.partial(k2_body, n), out_shape=[sds((nb, seq, d)...]
    dot_general x4 -> x0, matrix products: 250 us -> none  [the longest x1 81.7 us: local_layer(): jnp.einsum('cirl,ile->cre', attended, w_out, preferred_element_type=jnp.f...]
    reduce_sum x4 -> x0, other arithmetic: 103 us -> none  [the longest x2 66 us: layer_norm(): row_mean = jnp.mean(values, axis=-1, keepdims=True)]
    sub x1 -> x0, matrix products: 82.6 us -> none  [attend(): attn_probs = jax.nn.softmax(scores, axis=-1).astype(jnp.bfloat16)]
    convert_element_type x5 -> x0, other arithmetic: 49.8 us -> none  [the longest x1 49.2 us: local_layer(): (x_mid.astype(jnp.float32) + summed_down.astype(jnp.float32) + b_down.ast...]
    unnamed x32 -> x11, local copies, waits for them, and re-layouts: 1.89 us -> 33.4 us
    ppermute x0 -> x6, waiting for transfers between devices: none -> 18.6 us  [the longest x3 15.3 us: moved(): fr = [lax.ppermute(t, 'tp', left) for t in parts]]
  transfers between devices with their start and end apart: 2 -> 6, of which waited for: 2 -> 3; matrix products, arithmetic and copies ran while one was open for 1% -> 1% of each run, Pallas kernels for 0% -> 20%
where the time goes in v1:
time: 655 us; the launch traced here: 645 us
  Pallas kernels  572 us (87%)
  local copies, waits for them, and re-layouts  38.2 us (6%)
  waiting for transfers between devices  18.6 us (3%)
  starting transfers between devices  9.93 us (2%)
    pallas_call x1, Pallas kernels, k2(): pl.pallas_call(functools.partial(k2_body, n), out_shape=[sds((nb, seq, d)...  446 us
    pallas_call x1, Pallas kernels, k1(): pl.pallas_call(functools.partial(k1_body, hd, b0=0, ln_rows=ln_rows, qt=q...  126 us
    unnamed x11, local copies, waits for them, and re-layouts  33.4 us
    ppermute x3, waiting for transfers between devices, moved(): fr = [lax.ppermute(t, 'tp', left) for t in parts]  15.3 us
  transfers between devices with their start and end apart: 6, of which 3 were waited for; matrix products, arithmetic and copies ran while one was open for 1% of the time, Pallas kernels for 20%

profile of v1, /device:TPU:113, one launch (start us, length us, event | category | flops | bytes accessed | tf_op | source)
XLA Modules:
  0.0 644.8 jit_solution(17175167826667533166)
XLA Ops:
  0.6 0.0 slice-start
  0.6 3.8 collective-permute-start.5
  4.4 1.3 constant_dynamic-slice_fusion
  5.7 1.9 pad_maximum_fusion.1
  7.6 2.7 collective-permute-start.4
  10.3 0.0 collective-permute-start.1
  10.3 1.3 constant_dynamic-slice_fusion.1
  11.6 2.0 pad_maximum_fusion
  13.6 2.7 collective-permute-start.3
  16.3 0.7 slice.17.bq_ref
  17.0 0.9 reshape.66.bkv_ref
  17.9 8.4 %collective-permute-done.5.fro = bf16[256,2048]{1,0:T(8,128)(2,1)} collective-permute-done((bf16[256,2048]{1,0:T(8,128)(2,1)}, bf16[256,2048]{1,0:T(8,128)(2,1)}, u32[]{:S(2)}, u32[]{:S(2)}) %collective-permute-start.5) | collective-permute-done | bytes 1048608 | tf_op jit(solution)/shard_map/ppermute | solution.py:415
  26.3 0.8 collective-permute-start
  27.1 126.0 %shard_map.157 = (bf16[12,1024,256]{2,1,0:T(8,128)(2,1)}, bf16[12,256,1024]{2,1,0:T(8,128)(2,1)}, bf16[12,256,1024]{2,1,0:T(8,128)(2,1)}) custom-call(s32[12]{0:T(128)} %lens_ref.1, bf16[12,1024,2048]{2,1,0:T(8,128)(2,1)} %x_ref.3, f32[1,2048]{1,0:T(1,128)} %bitcast.22, f32[1,2048]{1,0:T(1,128)} %bitcast.23, bf16[768,2048]{1,0:T(8,128)(2,1)} %bitcast.18, ...), custom_call_target="tpu_custom_call" | custom-call | flops 45097156608 | bytes 69206016 | tf_op jit(solution)/shard_map/pallas_call | solution.py:75
  153.1 0.6 reshape.62
  153.7 0.6 reshape.64
  154.3 0.0 collective-permute-done.2.flo
  154.3 0.0 collective-permute-done.4.frd
  154.3 0.0 collective-permute-done.1.fld
  154.3 6.9 %collective-permute-done.3.fru = bf16[1536,1024]{1,0:T(8,128)(2,1)S(1)} collective-permute-done((bf16[1536,1024]{1,0:T(8,128)(2,1)}, bf16[1536,1024]{1,0:T(8,128)(2,1)S(1)}, u32[]{:S(2)}, u32[]{:S(2)}) %collective-permute-start.3) | collective-permute-done | bytes 3145760 | tf_op jit(solution)/shard_map/ppermute | solution.py:415
  161.2 3.3 collective-permute-done.flu
  164.4 0.6 broadcast_in_dim.2.bup_ref
  165.0 446.0 %shard_map.158 = (bf16[12,1024,2048]{2,1,0:T(8,128)(2,1)}, bf16[2,8,6,128,256]{4,3,2,1,0:T(8,128)(2,1)}, bf16[8,2048,1024]{2,1,0:T(8,128)(2,1)}, bf16[8,1024,2048]{2,1,0:T(8,128)(2,1)}, bf16[8,256,2048]{2,1,0:T(8,128)(2,1)}) custom-call(bf16[12,1024,256]{2,1,0:T(8,128)(2,1)} %get-tuple-element.7.a_ref, bf16[12,1024,2048]{2,1,0:T(8,128)(2,1)} %x_ref.3, ...), custom_call_target="tpu_custom_call" | custom-call | flops 115964116992 | bytes 134217728 | tf_op jit(solution)/shard_map/pallas_call | solution.py:388
  611.1 33.3 %copy.19 = bf16[12,1024,2048]{2,1,0:T(8,128)(2,1)} copy(bf16[12,1024,2048]{2,1,0:T(8,128)(2,1)} %get-tuple-element.14) | data formatting | bytes 100663296
  (16 shorter events, 0.0 us)
Async XLA Ops:
  0.6 5.1 slice-start
  0.6 25.7 %collective-permute-start.5 = (bf16[256,2048]{1,0:T(8,128)(2,1)}, bf16[256,2048]{1,0:T(8,128)(2,1)}, u32[]{:S(2)}, u32[]{:S(2)}) collective-permute-start(bf16[256,2048]{1,0:T(8,128)(2,1)} %bitcast.19), channel_id=1, source_target_pairs={{0,6},{1,7},{2,0},{3,1},{4,2},{5,3},{6,4},{7,5},{8,14},{9,15},{10,... | collective-permute-start | bytes 3145736 | tf_op jit(solution)/shard_map/ppermute | solution.py:415
  4.4 149.9 %collective-permute-start.2 = (bf16[256,2048]{1,0:T(8,128)(2,1)}, bf16[256,2048]{1,0:T(8,128)(2,1)}, u32[]{:S(2)}, u32[]{:S(2)}) collective-permute-start(bf16[256,2048]{1,0:T(8,128)(2,1)} %bitcast.20), channel_id=1, source_target_pairs={{0,2},{1,3},{2,4},{3,5},{4,6},{5,7},{6,0},{7,1},{8,10},{9,11},{10,... | collective-permute-start | bytes 3145736 | tf_op jit(solution)/shard_map/ppermute | solution.py:414
  7.6 4.0 slice-start.1
  7.6 146.7 %collective-permute-start.4 = (bf16[768,2048]{1,0:T(8,128)(2,1)}, bf16[768,2048]{1,0:T(8,128)(2,1)}, u32[]{:S(2)}, u32[]{:S(2)}) collective-permute-start(bf16[768,2048]{1,0:T(8,128)(2,1)} %pad_maximum_fusion.1), channel_id=1, source_target_pairs={{0,6},{1,7},{2,0},{3,1},{4,2},{5,3},{6,4},{7,5},{8,14},{9,15},{10,... | collective-permute-start | bytes 9437192 | tf_op jit(solution)/shard_map/ppermute | solution.py:415
  10.3 144.0 %collective-permute-start.1 = (bf16[768,2048]{1,0:T(8,128)(2,1)}, bf16[768,2048]{1,0:T(8,128)(2,1)}, u32[]{:S(2)}, u32[]{:S(2)}) collective-permute-start(bf16[768,2048]{1,0:T(8,128)(2,1)} %pad_maximum_fusion.1), channel_id=1, source_target_pairs={{0,2},{1,3},{2,4},{3,5},{4,6},{5,7},{6,0},{7,1},{8,10},{9,11},{10,... | collective-permute-start | bytes 9437192 | tf_op jit(solution)/shard_map/ppermute | solution.py:414
  10.3 6.0 copy-start
  13.6 147.5 %collective-permute-start.3 = (bf16[1536,1024]{1,0:T(8,128)(2,1)}, bf16[1536,1024]{1,0:T(8,128)(2,1)S(1)}, u32[]{:S(2)}, u32[]{:S(2)}) collective-permute-start(bf16[1536,1024]{1,0:T(8,128)(2,1)} %pad_maximum_fusion), channel_id=1, source_target_pairs={{0,6},{1,7},{2,0},{3,1},{4,2},{5,3},{6,4},{7,5},{8,14},{9,15},{10,... | collective-permute-start | bytes 9437192 | tf_op jit(solution)/shard_map/ppermute | solution.py:415
  26.3 138.1 %collective-permute-start = (bf16[1536,1024]{1,0:T(8,128)(2,1)}, bf16[1536,1024]{1,0:T(8,128)(2,1)}, u32[]{:S(2)}, u32[]{:S(2)}) collective-permute-start(bf16[1536,1024]{1,0:T(8,128)(2,1)} %pad_maximum_fusion), channel_id=1, source_target_pairs={{0,2},{1,3},{2,4},{3,5},{4,6},{5,7},{6,0},{7,1},{8,10},{9,11},{10,... | collective-permute-start | bytes 9437192 | tf_op jit(solution)/shard_map/ppermute | solution.py:414
  27.1 126.0 %copy-start.1 = (bf16[2048]{0:T(1024)(128)(2,1)S(1)}, bf16[2048]{0:T(1024)(128)(2,1)}, u32[]{:S(2)}) copy-start(bf16[2048]{0:T(1024)(128)(2,1)} %param.21) | copy-start | bytes 12292
  27.1 126.6 %copy-start.2 = (bf16[2048]{0:T(1024)(128)(2,1)S(1)}, bf16[2048]{0:T(1024)(128)(2,1)}, u32[]{:S(2)}) copy-start(bf16[2048]{0:T(1024)(128)(2,1)} %param.27) | copy-start | bytes 12292
  27.1 137.3 %copy-start.3 = (bf16[1024]{0:T(1024)(128)(2,1)S(1)}, bf16[1024]{0:T(1024)(128)(2,1)}, u32[]{:S(2)}) copy-start(bf16[1024]{0:T(1024)(128)(2,1)} %param.25) | copy-start | bytes 6148
  161.1 3.9 copy-start.4

commit v2 on v0

v2 whole, which is shorter than its diff:
```python
import functools
import math

import jax
import jax.numpy as jnp
from jax import lax
from jax.experimental import pallas as pl
from jax.experimental.pallas import tpu as pltpu
from jax.sharding import PartitionSpec as P

F32 = jnp.float32
BF16 = jnp.bfloat16
NT = (((1,), (1,)), ((), ()))
MESH = pl.DeviceIdType.MESH


def norm(x, gain, bias):
    mu = jnp.mean(x, axis=-1, keepdims=True)
    c = x - mu
    var = jnp.mean(c * c, axis=-1, keepdims=True)
    return (c * lax.rsqrt(var + 1e-5) * gain + bias).astype(BF16)


def attention_rows(hd, qt, length, x_ref, h_scr, wt_ref, g_ref, bt_ref, bq_ref, bkv_ref, a_ref, kv_ref, q_scr, ka_scr, kb_scr):
    seq, width = a_ref.shape
    n_heads = width // hd
    rows = seq // 4
    for r in range(4):
        h_scr[r * rows:(r + 1) * rows, :] = norm(x_ref[r * rows:(r + 1) * rows, :].astype(F32), g_ref[...], bt_ref[...])
    q = lax.dot_general(h_scr[...], wt_ref[:width, :], NT, preferred_element_type=F32)
    q_scr[...] = (q + bq_ref[...]).astype(BF16)
    keep = lax.broadcasted_iota(jnp.int32, (width, seq), 1) < length
    kt = lax.dot_general(wt_ref[width:2 * width, :], h_scr[...], NT, preferred_element_type=F32)
    kt = jnp.where(keep, kt + bkv_ref[:width, :], 0.0).astype(BF16)
    kv_ref[:width, :] = kt
    row = lax.broadcasted_iota(jnp.int32, (width, seq), 0)
    bias = jnp.where(keep, 0.0, -1e30).astype(BF16)
    ka_scr[...] = jnp.where(row == width - 1, bias, kt)
    kb_scr[...] = jnp.where(row == 0, bias, kt)
    vt = lax.dot_general(wt_ref[2 * width:, :], h_scr[...], NT, preferred_element_type=F32)
    kv_ref[width:, :] = jnp.where(keep, vt + bkv_ref[width:, :], 0.0).astype(BF16)

    c2 = hd ** -0.5 * math.log2(math.e)
    lane = lax.broadcasted_iota(jnp.int32, (qt, width), 1)
    causal = lax.broadcasted_iota(jnp.int32, (qt, qt), 1) <= lax.broadcasted_iota(jnp.int32, (qt, qt), 0)
    for i in range(seq // qt):
        span = (i + 1) * qt
        q_tile = q_scr[i * qt:(i + 1) * qt, :]
        out = jnp.zeros((qt, width), F32)
        for h in range(n_heads):
            low = h < n_heads // 2
            mine = (lane >= h * hd) & (lane < (h + 1) * hd)
            flag = lane == (width - 1 if low else 0)
            qm = jnp.where(mine, q_tile, jnp.where(flag, 1.0, 0.0).astype(BF16))
            k_src = ka_scr if low else kb_scr
            s = jnp.dot(qm, k_src[:, :span], preferred_element_type=F32)
            s_diag = jnp.where(causal, s[:, span - qt:], -1e30)
            s = jnp.concatenate([s[:, :span - qt], s_diag], axis=1) if i else s_diag
            m = jnp.max(s, axis=-1, keepdims=True)
            p = jnp.exp2((s - m) * c2)
            total = jnp.sum(p, axis=-1, keepdims=True)
            p = (p * (1.0 / total)).astype(BF16)
            pv = lax.dot_general(p, kv_ref[width:, :span], NT, preferred_element_type=F32)
            out = jnp.where(mine, pv, out)
        a_ref[i * qt:(i + 1) * qt, :] = out.astype(BF16)


def layer_body(n, hd, lens_ref, x_ref, wt_in, wu_in, wd_in, wo_in, bias_ref, g1_ref, t1_ref, g2_ref, t2_ref,
               out_ref, a_hbm, kc_hbm, vc_hbm, aall, wu, wd, wo,
               acc, h2, stage, ubuf, wub, wdb, abuf, wob, bups, bkv_ref, q_scr, ka_scr, kb_scr, ao, kvo,
               send_sems, recv_sems, sem_u, sem_d, sem_a, sem_o, sem_x, sem_k, sem_g, sem_w):
    nb, seq, d = x_ref.shape
    ff = wu_in.shape[1]
    width = wo_in.shape[0]
    rb = seq // n
    hb = nb // 2
    hr = hb * rb
    bo_ref, bd_ref = bias_ref.at[:, :d], bias_ref.at[:, d:2 * d]
    bq_ref = bias_ref.at[:, 2 * d + ff:2 * d + ff + width]
    me = lax.axis_index("tp")
    dp = lax.axis_index("dp")
    par = lax.rem(dp, 2)
    flip = 1 - 2 * lax.rem(me, 2)
    rgt, lft, opp = lax.rem(me + 2, n), lax.rem(me + n - 2, n), lax.rem(me + n // 2, n)
    sib, lft2, rgt2, opp2 = me + flip, lft + flip, rgt + flip, opp + flip
    to_r, to_l, to_s = {"tp": rgt}, {"tp": lft}, {"tp": sib}
    to_p = {"dp": dp + 1 - 2 * par}
    scope = jax.named_scope

    barrier = pltpu.get_barrier_semaphore()
    for r in range(1, n):
        pl.semaphore_signal(barrier, inc=1, device_id={"tp": lax.rem(me + r, n)}, device_id_type=MESH)
    pl.semaphore_signal(barrier, inc=1, device_id=to_p, device_id_type=MESH)
    pl.semaphore_wait(barrier, n)

    copies, got = [], set()

    def remote(src, dst, target):
        i = len(copies)
        c = pltpu.make_async_remote_copy(src_ref=src, dst_ref=dst, send_sem=send_sems.at[i], recv_sem=recv_sems.at[i], device_id=target, device_id_type=MESH)
        copies.append(c)
        return c

    def pieces(ref, names, target, at=None):
        pass

    def start(*cs):
        for c in cs:
            c.start()

    def ensure(*cs):
        for c in cs:
            if id(c) not in got:
                got.add(id(c))
                c.wait_recv()

    uw, cw = ff // 4, 3 * ff // 8
    pc, qc = pl.multiple_of(uw + par * cw, 128), pl.multiple_of(uw + (1 - par) * cw, 128)
    po, qo = pl.multiple_of(par * (width // 2), width // 2), pl.multiple_of((1 - par) * (width // 2), width // 2)
    dh = d // 2
    ua, ub = pl.ds(0, uw // 2), pl.ds(uw // 2, uw // 2)
    part_cols = {"u": pl.ds(0, uw), "p": pl.ds(pc, cw), "q": pl.ds(qc, cw)}
    rows_of = {"": pl.ds(0, d), "a": pl.ds(0, dh), "b": pl.ds(dh, dh)}

    def down_rows(share, half):
        base, size = {"u": (0, uw), "p": (pc, cw), "q": (qc, cw)}[share]
        if half == "":
            return pl.ds(base, size)
        off = base + (size // 2 if half == "b" else 0)
        return pl.ds(off if share == "u" else pl.multiple_of(off, 64), size // 2)

    def out_rows(share, half):
        base, size = {"p": po, "q": qo}[share], width // 2
        if half == "":
            return pl.ds(base, size)
        return pl.ds(pl.multiple_of(base + (size // 2 if half == "b" else 0), size // 2), size // 2)

    def view(kind, slot, share, half):
        if kind == "up":
            ref = wu_in if slot is None else wu.at[slot]
            return ref.at[rows_of[half], part_cols[share]]
        if kind == "dn":
            ref = wd_in if slot is None else wd.at[slot]
            return ref.at[down_rows(share, half), :]
        ref = wo_in if slot is None else wo.at[slot]
        return ref.at[out_rows(share, half), :]

    own, fwd, pair, sb = {}, {}, {}, {}
    halves = [("up", "p"), ("dn", "p"), ("up", "u"), ("dn", "u")]
    for side, target in (("R", to_r), ("L", to_l)):
        own[side, "wo", "p", ""] = remote(view("wo", None, "p", ""), view("wo", me, "p", ""), target)
        for kind, share in halves:
            for half in "ab":
                own[side, kind, share, half] = remote(view(kind, None, share, half), view(kind, me, share, half), target)
    for side, target, half, held in (("R", to_r, "a", lft), ("L", to_l, "b", rgt)):
        for kind, share in [("wo", "p")] + halves:
            fwd[side, kind, share] = remote(view(kind, held, share, half), view(kind, held, share, half), target)
    for name, held in (("lft", lft), ("rgt", rgt), ("opp", opp)):
        pair[name, "wo", ""] = remote(view("wo", held, "p", ""), view("wo", held, "p", ""), to_p)
        for kind in ("up", "dn"):
            for half in "ab":
                pair[name, kind, half] = remote(view(kind, held, "p", half), view(kind, held, "p", half), to_p)
        for kind, share in [("wo", "p"), ("wo", "q"), ("up", "p"), ("up", "q"), ("dn", "p"), ("dn", "q"), ("up", "u"), ("dn", "u")]:
            sb[name, kind, share] = remote(view(kind, held, share, ""), view(kind, held, share, ""), to_s)
    sb["own", "wo"] = remote(wo_in, wo.at[me], to_s)
    sb["own", "up"] = remote(wu_in, wu.at[me], to_s)
    sb["own", "dn"] = remote(wd_in, wd.at[me], to_s)
    bup = [remote(bups.at[me], bups.at[me], {"tp": lax.rem(me + r, n)}) for r in range(1, n)]
    a2a = {}
    for h in (0, 1):
        for r, t in enumerate((sib, rgt, lft, rgt2, lft2, opp, opp2)):
            a2a[h, r] = remote(a_hbm.at[h * hb:(h + 1) * hb, pl.ds(pl.multiple_of(t * rb, rb), rb), :], aall.at[h, me], {"tp": t})

    def at_out(h, b, owner):
        return out_ref.at[h * hb + b, pl.ds(pl.multiple_of(owner * rb, rb), rb), :]
    cut = hb // 2
    first = list(range(hb))
    other = first[cut:] + first[:cut]
    xo, xf, xs = {}, {}, {}
    for h in (0, 1):
        for b in range(hb):
            for side, target in (("R", to_r), ("L", to_l), ("S", to_s)):
                xo[h, b, side] = remote(stage.at[h, b], at_out(h, b, me), target)
            held, target = (lft, to_r) if b < cut else (rgt, to_l)
            xf[h, b] = remote(at_out(h, b, held), at_out(h, b, held), target)
            for name, held in (("lft", lft), ("rgt", rgt), ("opp", opp)):
                xs[h, b, name] = remote(at_out(h, b, held), at_out(h, b, held), to_s)

    src_of = {"lft": "R", "rgt": "L"}

    def got_wo():
        ensure(own["R", "wo", "p", ""], own["L", "wo", "p", ""])
        start(pair["lft", "wo", ""], pair["rgt", "wo", ""], fwd["R", "wo", "p"], fwd["L", "wo", "p"], sb["lft", "wo", "p"], sb["rgt", "wo", "p"])

    def got_first(kind):
        ensure(own["R", kind, "p", "a"], own["L", kind, "p", "b"])
        start(fwd["R", kind, "p"], fwd["L", kind, "p"], pair["lft", kind, "a"])
        if kind == "up":
            start(pair["rgt", kind, "b"])

    def got_second(kind):
        ensure(own["R", kind, "p", "b"], own["L", kind, "p", "a"])
        start(pair["lft", kind, "b"])
        if kind == "dn":
            start(pair["rgt", kind, "b"])
        start(pair["rgt", kind, "a"], sb["lft", kind, "p"], sb["rgt", kind, "p"])

    def got_opp(kind):
        ensure(fwd["R", kind, "p"], fwd["L", kind, "p"])
        if kind == "wo":
            start(pair["opp", "wo", ""])
        else:
            start(pair["opp", kind, "a"], pair["opp", kind, "b"])
        start(sb["opp", kind, "p"])

    def got_pair(name, kind):
        ensure(*[pair[name, kind, half] for half in ([""] if kind == "wo" else "ab")])
        start(sb[name, kind, "q"])

    def got_u(kind):
        ensure(own["R", kind, "u", "a"], own["L", kind, "u", "b"])
        start(fwd["R", kind, "u"], fwd["L", kind, "u"])
        ensure(own["R", kind, "u", "b"], own["L", kind, "u", "a"])
        start(sb["lft", kind, "u"], sb["rgt", kind, "u"])

    def got_opp_u(kind):
        ensure(fwd["R", kind, "u"], fwd["L", kind, "u"])
        start(sb["opp", kind, "u"])

    def send_own(kind, share):
        start(own["R", kind, share, "a"], own["L", kind, share, "b"], own["R", kind, share, "b"], own["L", kind, share, "a"])

    start(own["R", "wo", "p", ""], own["L", "wo", "p", ""])
    send_own("up", "p")
    wt_copy = pltpu.make_async_copy(wt_in, abuf, sem_w.at[0])
    wt_copy.start()

    def x_copy(b, slot):
        return pltpu.make_async_copy(x_ref.at[b], wdb.at[slot], sem_x.at[slot])
    x_copy(0, 0).start()
    start(sb["own", "wo"], sb["own", "up"], sb["own", "dn"])
    bups[me] = jnp.broadcast_to(bias_ref[:, 2 * d:2 * d + ff], (8, ff))
    bkv_ref[...] = jnp.transpose(jnp.broadcast_to(bias_ref[:, 2 * d + ff + width:], (8, 2 * width)))[:, :1]
    my_rows = pl.ds(pl.multiple_of(me * rb, rb), rb)
    own_x = [pltpu.make_async_copy(x_ref.at[h * hb:(h + 1) * hb, my_rows, :], stage.at[h], sem_g.at[h]) for h in (0, 1)]
    wt_copy.wait()

    def put_outs(b, slot):
        return [pltpu.make_async_copy(ao.at[slot], a_hbm.at[b], sem_k.at[slot, 0]), pltpu.make_async_copy(kvo.at[slot, :width], kc_hbm.at[b], sem_k.at[slot, 1]),
                pltpu.make_async_copy(kvo.at[slot, width:], vc_hbm.at[b], sem_k.at[slot, 2])]

    def wo_load(j, i):
        src = wo_in if i == 0 else wo.at[j]
        return pltpu.make_async_copy(src, wob.at[pl.ds(pl.multiple_of(j * width, width), width)], sem_o.at[i])
    wo_loads = [wo_load(j, i) for i, j in enumerate((me, sib, lft, lft2, rgt, rgt2, opp, opp2))]

    def early():
        wo_loads[0].start()
        start(*bup)
        start(*own_x)

    def near_wo():
        got_pair("lft", "wo")
        got_pair("rgt", "wo")

    events = {
        0: [got_wo, early],
        2: [lambda: got_first("up"), lambda: send_own("dn", "p")],
        4: [lambda: got_opp("wo"), lambda: got_second("up"), near_wo],
        6: [lambda: start(*[a2a[0, r] for r in range(n - 1)]), lambda: got_opp("up")],
        7: [lambda: got_first("dn"), lambda: send_own("up", "u"), lambda: send_own("dn", "u")],
        9: [lambda: got_second("dn"), lambda: got_pair("opp", "wo")],
        11: [lambda: got_pair("lft", "up"), lambda: got_pair("rgt", "up")],
    }

    @pl.loop(0, nb)
    def _(b):
        slot = lax.rem(b, 2)
        x_copy(b, slot).wait()

        @pl.when(b + 1 < nb)
        def _():
            x_copy(b + 1, 1 - slot).start()
        with scope("attention"):
            attention_rows(hd, min(256, seq), lens_ref[b], wdb.at[slot], h2, abuf, g1_ref, t1_ref, bq_ref, bkv_ref, ao.at[slot], kvo.at[slot], q_scr, ka_scr, kb_scr)
        for c in put_outs(b, slot):
            c.start()

        @pl.when(b > 0)
        def _():
            for c in put_outs(b - 1, 1 - slot):
                c.wait()
        for k, todo in events.items():
            @pl.when(b == k)
            def _(k=k, todo=todo):
                with scope("event%d" % k):
                    for e in todo:
                        e()
    for c in put_outs(nb - 1, (nb - 1) % 2):
        c.wait()

    def shard_at(k, other):
        return lax.rem(me + 3 * k * (k + 1), n) + other * flip

    tile = 256

    def whole(j, slot):
        return [pltpu.make_async_copy(wu.at[j], wub.at[slot], sem_u.at[slot]), pltpu.make_async_copy(wd.at[j], wdb.at[slot], sem_d.at[slot])]

    def own_whole(slot):
        return [pltpu.make_async_copy(wu_in, wub.at[slot], sem_u.at[slot]), pltpu.make_async_copy(wd_in, wdb.at[slot], sem_d.at[slot])]

    def load_shares(j, shares, slot):
        at = 0
        for share in shares:
            size = uw if share == "u" else cw
            pltpu.make_async_copy(view("up", j, share, ""), wub.at[slot, :, at:at + size], sem_u.at[slot]).start()
            pltpu.make_async_copy(view("dn", j, share, ""), wdb.at[slot, at:at + size], sem_d.at[slot]).start()
            at += size

    def mlp(j, shares, slot):
        if shares == "all":
            spans = [(c, slice(c, c + tile), tile) for c in range(0, ff, tile)]
        else:
            spans, at = [], 0
            for share in shares:
                base, size = {"u": (0, uw), "p": (pc, cw), "q": (qc, cw)}[share]
                spans.append((at, pl.ds(base, size), size))
                at += size
        size = sum(w for _, _, w in spans)
        pltpu.make_async_copy(wu.at[0, :, :size], wub.at[slot, :, :size], sem_u.at[slot]).wait()
        for at, cols, w in spans:
            u = jnp.dot(h2[:hr], wub[slot, :, at:at + w], preferred_element_type=F32)
            ubuf[:, at:at + w] = jnp.maximum(u + bups[j, 0:1, cols], 0.0).astype(BF16)
        pltpu.make_async_copy(wd.at[0, :size], wdb.at[slot, :size], sem_d.at[slot]).wait()
        for c in range(0, d, tile):
            acc[:, c:c + tile] += jnp.dot(ubuf[:, :size], wdb[slot, :size, c:c + tile], preferred_element_type=F32)

    def load_a(h):
        def put(src, j, i):
            for b in range(hb):
                c = pltpu.make_async_copy(src.at[b], abuf.at[b * rb:(b + 1) * rb, pl.ds(pl.multiple_of(j * width, width), width)], sem_a.at[i])
                c.start()
                yield c
        cs = list(put(a_hbm.at[h * hb:(h + 1) * hb, my_rows, :], me, 0))
        for r, j in enumerate((sib, lft, rgt, lft2, rgt2, opp, opp2)):
            ensure(a2a[h, r])
            cs += list(put(aall.at[h, j], j, r + 1))
        for i in range(n):
            pltpu.make_async_copy(aall.at[h, i], aall.at[h, i], sem_a.at[i]).wait()

    def proj(h):
        own_x[h].wait() if h == 0 else None
        @pl.loop(0, d // tile, unroll=PROJ_UNROLL)
        def _(i):
            cols = pl.ds(pl.multiple_of(i * tile, tile), tile)
            acc[:, cols] = jnp.dot(abuf[...], wob[:, cols], preferred_element_type=F32)
        @pl.loop(0, hb)
        def _(b):
            rows = pl.ds(pl.multiple_of(b * rb, rb), rb)
            x1 = (stage[h, b].astype(F32) + acc[rows, :] + bo_ref[...]).astype(BF16).astype(F32)
            h2[rows, :] = norm(x1, g2_ref[...], t2_ref[...])
            acc[rows, :] = x1 + bd_ref[...]

    put_own = [pltpu.make_async_copy(stage.at[h], out_ref.at[h * hb:(h + 1) * hb, my_rows, :], sem_g.at[h]) for h in (0, 1)]

    def finish(h):
        for b in range(hb):
            stage[h, b] = acc[b * rb:(b + 1) * rb, :].astype(BF16)
        put_own[h].start()
        for b1, b2 in zip(first, other):
            start(xo[h, b1, "R"], xo[h, b2, "L"])
        start(*[xo[h, b, "S"] for b in range(hb)])

    def pass_on(h, b, side):
        ensure(xo[h, b, side])
        if (b < cut) == (side == "R"):
            start(xf[h, b])
        start(xs[h, b, "lft" if side == "R" else "rgt"])

    def relay(h, i):
        pass_on(h, first[i], "R")
        pass_on(h, other[i], "L")

    def last(h, b):
        ensure(xf[h, b])
        start(xs[h, b, "opp"])

    with scope("wo_loads"):
        ensure(sb["own", "wo"])
        for name in ("lft", "rgt"):
            ensure(sb[name, "wo", "p"], sb[name, "wo", "q"])
        start(*wo_loads[1:6])
        ensure(sb["opp", "wo", "p"], sb["opp", "wo", "q"])
        start(*wo_loads[6:])
        ensure(*bup)
        own_x[1].wait()
    start(*own_whole(0))
    ensure(sb["own", "up"], sb["own", "dn"])
    start(*whole(sib, 1))
    with scope("load_a0"):
        load_a(0)
    with scope("wo_wait"):
        for c in wo_loads:
            c.wait()
    with scope("proj0"):
        proj(0)

    def need(*keys):
        ensure(*[sb[k] for k in keys])

    def sib_keys(name, shares):
        return [(name, kind, share) for kind in ("up", "dn") for share in shares]

    def opposite(shares):
        load_shares(opp, shares, 0)

        @pl.loop(0, 2)
        def _(t):
            @pl.when(t == 0)
            def _():
                need(*sib_keys("opp", shares))
                load_shares(opp2, shares, 1)
            with scope("mlp_" + shares):
                mlp(shard_at(3, t), shares, t)

    def end_of_first_half():
        with scope("arrive_opp_up"):
            got_opp_u("up")
            got_opp_u("dn")
        opposite("pu")
        with scope("arrive_opp_q"):
            got_pair("opp", "dn")
        opposite("q")
        with scope("fin0"):
            finish(0)
        start(*own_whole(0))
        start(*whole(sib, 1))
        with scope("load_a1"):
            load_a(1)
        with scope("proj1"):
            proj(1)

    def arrive_lft():
        got_opp("dn")
        got_pair("opp", "up")
        got_u("up")
        got_u("dn")
        start(*[a2a[1, r] for r in range(n - 1)])
        got_pair("lft", "dn")
        start(*whole(lft, 0))
        need(*sib_keys("lft", "upq"))
        start(*whole(lft2, 1))

    def arrive_rgt():
        got_pair("rgt", "dn")
        start(*whole(rgt, 0))

    def arrive_rgt2():
        need(*sib_keys("rgt", "upq"))
        start(*whole(rgt2, 1))

    steps = n - 2
    first_events = {1: arrive_lft, 3: arrive_rgt, 4: arrive_rgt2, 5: end_of_first_half}

    @pl.loop(0, steps + n)
    def _(s):
        r = s - steps * lax.div(s + n - steps, n)
        slot = lax.rem(s, 2)
        with scope("mlp"):
            mlp(shard_at(lax.div(r, 2), slot), "all", slot)
        for k, event in first_events.items():
            @pl.when(s == k)
            def _(k=k, event=event):
                with scope("first%d" % k):
                    event()
        for k in range(hb):
            @pl.when(s == k + steps + 1)
            def _(k=k):
                with scope("relay0_%d" % k):
                    relay(0, k)

        @pl.when((s >= steps) & (s < steps + n - 2))
        def _():
            start(*whole(shard_at(lax.div(r, 2) + 1, slot), slot))
    with scope("fin1"):
        finish(1)
    for i in range(hb):
        with scope("relay1_%d" % i):
            relay(1, i)
    for h in (0, 1):
        for i in range(cut):
            with scope("last%d_%d" % (h, i)):
                last(h, i)
                last(h, cut + i)
    with scope("final"):
        for h in (0, 1):
            put_own[h].wait()
        ensure(*copies)
        for c in copies:
            c.wait_send()


N_COPIES = 192
PROJ_UNROLL = 2


def layer(n, x_in, seq_lens, g1, t1, w_qkv, b_qkv, w_out, b_out, g2, t2, w_up, b_up, w_down, b_down):
    nb, seq, d = x_in.shape
    _, _, nh, hd = w_qkv.shape
    width = nh * hd
    ff = w_up.shape[1]
    rb, hb = seq // n, nb // 2
    hr = rb * hb
    wt = jnp.transpose(w_qkv, (1, 2, 3, 0)).reshape(3 * width, d)
    bias = jnp.concatenate([t.reshape(1, -1) for t in (b_out, b_down, b_up, b_qkv)], axis=1).astype(F32)
    any_ = pl.BlockSpec(memory_space=pl.ANY)
    vm = pl.BlockSpec(memory_space=pltpu.VMEM)
    row = lambda t: t.astype(F32).reshape(1, -1)
    sds = lambda *shape: jax.ShapeDtypeStruct(shape, BF16)
    dma = lambda *shape: pltpu.SemaphoreType.DMA(shape)
    outs = pl.pallas_call(
        functools.partial(layer_body, n, hd),
        out_shape=[sds(nb, seq, d), sds(nb, seq, width), sds(nb, width, seq), sds(nb, width, seq), sds(2, n, hb, rb, width), sds(n, d, ff), sds(n, ff, d), sds(n, width, d)],
        in_specs=[pl.BlockSpec(memory_space=pltpu.SMEM)] + [any_] * 5 + [vm] * 5,
        out_specs=[any_] * 8,
        scratch_shapes=[
            pltpu.VMEM((hr, d), F32), pltpu.VMEM((seq, d), BF16), pltpu.VMEM((2, hb, rb, d), BF16), pltpu.VMEM((hr, ff), BF16),
            pltpu.VMEM((2, d, ff), BF16), pltpu.VMEM((2, ff, d), BF16), pltpu.VMEM((hr, n * width), BF16), pltpu.VMEM((n * width, d), BF16),
            pltpu.VMEM((n, 8, ff), F32), pltpu.VMEM((2 * width, 1), F32), pltpu.VMEM((seq, width), BF16), pltpu.VMEM((width, seq), BF16), pltpu.VMEM((width, seq), BF16),
            pltpu.VMEM((2, seq, width), BF16), pltpu.VMEM((2, 2 * width, seq), BF16),
            dma(N_COPIES), dma(N_COPIES), dma(2), dma(2), dma(n), dma(n), dma(2), dma(2, 3), dma(2), dma(1),
        ],
        compiler_params=pltpu.CompilerParams(collective_id=0, has_side_effects=True, vmem_limit_bytes=63 * 2**20 + 2**19),
        cost_estimate=pl.CostEstimate(flops=2 * nb * seq * d * 3 * width + nb * rb * d * (4 * ff * n + 2 * n * width), bytes_accessed=8 * n * d * ff, transcendentals=nb * nh * seq * seq // 2),
    )(seq_lens, x_in, wt, w_up, w_down, w_out.reshape(width, d), bias, row(g1), row(t1), row(g2), row(t2))
    un = lambda t: jnp.transpose(t.reshape(nb, nh, hd, seq), (0, 1, 3, 2))
    return outs[0], un(outs[2]), un(outs[3])


def solution(mesh):
    n = mesh.shape["tp"]
    arg_specs = (P("dp", None, None), P("dp"), P(), P(), P(None, None, "tp", None), P(None, "tp", None), P("tp", None, None), P(), P(), P(), P(None, "tp"), P("tp"), P("tp", None), P())
    cache_spec = P("dp", "tp", None, None)
    result_specs = (P("dp", None, None), cache_spec, cache_spec)
    return jax.shard_map(functools.partial(layer, n), mesh=mesh, in_specs=arg_specs, out_specs=result_specs, check_vma=False)
```

time: 1490 us -> 531 us (0.36)
  waiting for transfers between devices: 970 us -> 0 us
  Pallas kernels: 0 us -> 484 us
  matrix products: 333 us -> 0 us
  other arithmetic: 172 us -> 0.63 us
  local copies, waits for them, and re-layouts: 1.89 us -> 45.8 us
    psum x2 -> x0, waiting for transfers between devices: 970 us -> none  [the longest x1 491 us: local_layer(): summed_out = lax.psum(part_out, 'tp')]
    pallas_call x0 -> x1, Pallas kernels: none -> 484 us  [layer(): pl.pallas_call(functools.partial(layer_body, n, hd), out_shape=[sds(nb, s...]
    dot_general x4 -> x0, matrix products: 250 us -> none  [the longest x1 81.7 us: local_layer(): jnp.einsum('cirl,ile->cre', attended, w_out, preferred_element_type=jnp.f...]
    reduce_sum x4 -> x0, other arithmetic: 103 us -> none  [the longest x2 66 us: layer_norm(): row_mean = jnp.mean(values, axis=-1, keepdims=True)]
    sub x1 -> x0, matrix products: 82.6 us -> none  [attend(): attn_probs = jax.nn.softmax(scores, axis=-1).astype(jnp.bfloat16)]
    convert_element_type x5 -> x1, other arithmetic: 49.8 us -> 0.63 us  [layer(): jnp.concatenate([t.reshape(1, -1) for t in (b_out, b_down, b_up, b_qkv)],...]
    unnamed x32 -> x5, local copies, waits for them, and re-layouts: 1.89 us -> 42.9 us
  transfers between devices with their start and end apart: 2 -> 0, of which waited for: 2 -> 0; matrix products, arithmetic and copies ran while one was open for 1% -> 0% of each run, Pallas kernels for 0% -> 0%
where the time goes in v2:
time: 531 us
  Pallas kernels  484 us (91%)
  local copies, waits for them, and re-layouts  45.8 us (9%)
    pallas_call x1, Pallas kernels, layer(): pl.pallas_call(functools.partial(layer_body, n, hd), out_shape=[sds(nb, s...  484 us
    unnamed x5, local copies, waits for them, and re-layouts  42.9 us

profile of v2, /device:TPU:113, one launch (start us, length us, event | category | flops | bytes accessed | tf_op | source)
XLA Modules:
  0.0 530.7 jit_solution(6825690980158099525)
XLA Ops:
  0.6 0.8 concatenate.22
  1.4 0.7 concatenate.21
  2.1 0.7 concatenate.19
  2.8 0.7 concatenate.20
  3.5 0.6 maximum_convert_fusion.bias_ref
  4.1 483.7 %shard_map.157 = (bf16[12,1024,2048]{2,1,0:T(8,128)(2,1)}, bf16[12,1024,256]{2,1,0:T(8,128)(2,1)}, bf16[12,256,1024]{2,1,0:T(8,128)(2,1)}, bf16[12,256,1024]{2,1...) custom-call(s32[12]{0:T(128)} %lens_ref.1, ...), custom_call_target="tpu_custom_call" | custom-call | flops 154618822656 | bytes 134217728 | tf_op jit(solution)/shard_map/pallas_call | solution.py:522
  487.8 33.3 %copy.20 = bf16[12,1024,2048]{2,1,0:T(8,128)(2,1)} copy(bf16[12,1024,2048]{2,1,0:T(8,128)(2,1)} %get-tuple-element.12) | data formatting | bytes 100663296
  521.1 0.0 copy-start
  521.1 6.9 %copy.21 = bf16[12,4,1024,64]{2,3,1,0:T(8,128)(2,1)} copy(bf16[12,4,1024,64]{2,3,1,0:T(8,128)(2,1)} %bitcast.15) | data formatting | bytes 12582912
  528.0 0.0 copy-done
  528.0 2.7 copy.22
Async XLA Ops:
  521.1 6.9 %copy-start = (bf16[12,256,1024]{2,1,0:T(8,128)(2,1)S(1)}, bf16[12,256,1024]{2,1,0:T(8,128)(2,1)}, u32[]{:S(2)}) copy-start(bf16[12,256,1024]{2,1,0:T(8,128)(2,1)} %get-tuple-element.8) | copy-start | bytes 18874372
